TPU v7x, 256 devices: a whole 4x4x8 slice. The times are simulated.
256 devices in a mesh: seq: 64 (over x, z_hi, y, core), head: 4 (over z_lo).
Axes of the slice: x: 4, y: 4, z: 8 (z_hi: 2, z_lo: 4; z = z_hi * 4 + z_lo), core: 2. Of those that a mesh axis runs over, the one named last changes fastest.
Arguments:
- span_order: int32 [128], replicated, may hold values from 0 to 127, each once
- queries: bfloat16 [8192, 36864], P('seq', 'head'), may hold values from -32 to 32
- latent_kv: bfloat16 [8192, 576], P(('seq', 'head')), may hold values from -8 to 8
- w_uv: bfloat16 [64, 512, 128], P('head'), may hold values from -0.25 to 0.25
Outputs:
- attended: bfloat16 [8192, 8192], P('seq', 'head')
Inputs may be any that keep to these rules, and one draw needn't show every extreme that they name: `span_order`: each of 0 to 127 appears once.
All inputs are finite; a program needn't handle non-finite values.
Results may differ from a plain program's by a relative error of at most 0.0065.
Values may be sent and summed in bfloat16 or wider, within the bound.
No kernel may reach another device: no remote copies, remote signals or barrier semaphores. Data moves between devices by JAX's collectives and lax.ppermute only.
A program may use at most 128 MiB of HBM per device.

v0:
```python
import math
import jax
import jax.numpy as jnp
from jax import lax
from jax.sharding import PartitionSpec as P

ROPE_DIM = 64
NOPE_DIM = 128
SEQS = 2
theta_base = 10000.0
floor_score = -1e30


def copy_for_each(shard, axis):
    copies = jnp.broadcast_to(shard, (lax.axis_size(axis), *shard.shape))
    return lax.all_to_all(copies, axis, split_axis=0, concat_axis=0, tiled=True)


def joined_along(tiles, dim):
    tiles = jnp.moveaxis(tiles, 0, dim)
    shape = tiles.shape
    return tiles.reshape(*shape[:dim], shape[dim] * shape[dim + 1], *shape[dim + 2 :])


def collect(shard, axis, dim):
    tiles = copy_for_each(shard, axis)
    return joined_along(tiles, dim)


def angle_tables(positions, half_width):
    inverse_freq = jnp.exp(
        -math.log(theta_base) * jnp.arange(half_width, dtype=jnp.float32) / half_width
    )
    phases = positions.astype(jnp.float32)[:, None] * inverse_freq[None, :]
    return (jnp.cos(phases), jnp.sin(phases))


def rotate(values, cosine, sine_table):
    half_width = values.shape[-1] // 2
    lower_part = values[..., :half_width]
    upper_part = values[..., half_width:]
    return jnp.concatenate(
        [
            lower_part * cosine - upper_part * sine_table,
            upper_part * cosine + lower_part * sine_table,
        ],
        -1,
    )


def unchanged(running):
    return running


def per_device(span_order, queries, latent_kv, w_uv):
    tok_dev = queries.shape[0]
    head_count = w_uv.shape[0]
    latent_rank = w_uv.shape[1]
    row_width = queries.shape[1] // head_count
    rope_width = row_width - latent_rank
    n_seq = lax.axis_size("seq")
    n_head = lax.axis_size("head")
    span_len = tok_dev // 2
    seq_len = tok_dev * n_seq // SEQS
    stream_ids = (
        span_order[:, None] * span_len + jnp.arange(span_len, dtype=jnp.int32)[None, :]
    ).reshape(-1)
    seq_of = stream_ids // seq_len
    pos_of = stream_ids % seq_len
    kv_count = latent_kv.shape[0]
    kv_first = (lax.axis_index("seq") * n_head + lax.axis_index("head")) * kv_count
    kv_pos = lax.dynamic_slice_in_dim(pos_of, kv_first, kv_count)
    cos_keys, sin_keys = angle_tables(kv_pos, rope_width // 2)
    key_rows = jnp.concatenate(
        [
            latent_kv[:, :latent_rank],
            rotate(latent_kv[:, latent_rank:].astype(jnp.float32), cos_keys, sin_keys).astype(
                jnp.bfloat16
            ),
        ],
        1,
    )
    query_first = lax.axis_index("seq") * tok_dev
    query_pos = lax.dynamic_slice_in_dim(pos_of, query_first, tok_dev)
    query_seq = lax.dynamic_slice_in_dim(seq_of, query_first, tok_dev)
    cos_query, sin_query = angle_tables(query_pos, rope_width // 2)
    query_grid = queries.reshape(tok_dev, head_count, row_width)
    rotated = rotate(
        query_grid[..., latent_rank:].astype(jnp.float32),
        cos_query[:, None, :],
        sin_query[:, None, :],
    ).astype(jnp.bfloat16)
    query_grid = jnp.concatenate([query_grid[..., :latent_rank], rotated], -1)
    query_blocks = (
        query_grid.reshape(2, span_len, head_count, row_width)
        .transpose(0, 2, 1, 3)
        .reshape(2, head_count * span_len, row_width)
    )
    span_pos = query_pos.reshape(2, span_len)
    span_seq = query_seq.reshape(2, span_len)[:, 0]
    logit_scale_factor = (NOPE_DIM + ROPE_DIM) ** (-0.5)
    group_rows = collect(key_rows, "head", 0)
    shard_rows = lax.all_gather(group_rows, "seq", axis=0, tiled=True)
    row_count = shard_rows.shape[0]
    maxima = jnp.full((2, head_count * span_len), floor_score, jnp.float32)
    totals = jnp.zeros((2, head_count * span_len), jnp.float32)
    weighted_sums = jnp.zeros((2, head_count * span_len, latent_rank), jnp.float32)
    new_maxima = []
    new_totals = []
    new_sums = []
    for half_index in range(2):
        visible = (seq_of[None, :] == span_seq[half_index]) & (
            pos_of[None, :] <= span_pos[half_index][:, None]
        )
        block_rows = query_blocks[half_index]

        def update(state_now, visible=visible, block_rows=block_rows):
            old_top, old_total, old_sum = state_now
            logit_scores = (
                lax.dot_general(
                    block_rows,
                    shard_rows,
                    (((1,), (1,)), ((), ())),
                    preferred_element_type=jnp.float32,
                )
                * logit_scale_factor
            )
            logit_scores = jnp.where(
                visible[None], logit_scores.reshape(head_count, span_len, row_count), -jnp.inf
            ).reshape(head_count * span_len, row_count)
            new_top = jnp.maximum(old_top, jnp.max(logit_scores, 1))
            expo = jnp.exp(logit_scores - new_top[:, None])
            new_total = jnp.sum(expo, 1)
            contrib = jnp.dot(
                expo.astype(jnp.bfloat16),
                shard_rows[:, :latent_rank],
                preferred_element_type=jnp.float32,
            )
            return (new_top, new_total, contrib)

        state_now = (maxima[half_index], totals[half_index], weighted_sums[half_index])
        state_now = lax.cond(jnp.any(visible), update, unchanged, state_now)
        new_maxima.append(state_now[0])
        new_totals.append(state_now[1])
        new_sums.append(state_now[2])
    running = (jnp.stack(new_maxima), jnp.stack(new_totals), jnp.stack(new_sums))
    maxima, totals, weighted_sums = running
    latent_out = (weighted_sums / totals[..., None]).astype(jnp.bfloat16)
    latent_out = latent_out.reshape(2, head_count, span_len, latent_rank)
    projected = jnp.einsum(
        "shcr,hrv->shcv", latent_out, w_uv, preferred_element_type=jnp.float32
    ).astype(jnp.bfloat16)
    return projected.transpose(0, 2, 1, 3).reshape(tok_dev, head_count * w_uv.shape[2])


def solution(mesh):
    in_specs = (P(), P("seq", "head"), P(("seq", "head"), None), P("head", None, None))
    out_specs = P("seq", "head")
    return jax.shard_map(
        per_device, mesh=mesh, in_specs=in_specs, out_specs=out_specs, check_vma=False
    )
```

profile of v0, /device:TPU:1, one launch (start us, length us, event | category | flops | bytes accessed | tf_op | source)
XLA Modules:
  0.0 265.8 jit_solution(6816313810189963737)
XLA Ops:
  6.5 0.8 slice_convert_fusion.1
  7.4 0.8 slice.65
  8.2 0.7 broadcast_multiply_fusion
  9.4 12.0 %all_to_all.5 = bf16[4,32,576]{2,1,0:T(8,128)(2,1)} all-to-all(bf16[4,32,576]{2,1,0:T(8,128)(2,1)S(1)} %broadcast_in_dim.44), channel_id=1, replica_groups=mesh['seq'=64,'head'=4] {'head'}, dimensions={0} | all-to-all | bytes 294912 | tf_op jit(solution)/shard_map/all_to_all | solution.py:16
  22.2 1.3 broadcast_compare_fusion
  23.5 2.6 fusion.34
  27.3 4.3 %copy.6 = bf16[128,9216]{0,1:T(8,128)(2,1)} copy(bf16[128,9216]{1,0:T(8,128)(2,1)} %param.9) | data formatting | bytes 4718592 | tf_op args[1]
  31.6 1.7 slice.73
  33.5 1.0 slice_convert_fusion
  34.6 1.6 pad_maximum_fusion
  36.2 4.9 %copy.7 = bf16[128,16,576]{2,1,0:T(8,128)(2,1)} copy(bf16[128,16,576]{0,2,1:T(8,128)(2,1)} %pad_maximum_fusion) | data formatting | bytes 4718592 | tf_op jit(solution)/shard_map/concatenate | solution.py:93
  41.1 105.8 %all-gather.2.cloned.1.call-done = bf16[8192,576]{1,0:T(8,128)(2,1)} async-done(((bf16[128,576]{1,0:T(8,128)(2,1)}), bf16[8192,576]{1,0:T(8,128)(2,1)}) %all-gather.2.cloned.1.call-update) | async-done | bytes 9437200 | tf_op jit(solution)/shard_map/all_gather | solution.py:103
  146.9 53.9 %conditional.2 = (f32[1,1024]{1,0:T(1,128)S(1)}, f32[1,16,64,512]{3,2,1,0:T(8,128)}) conditional(s32[]{:T(128)} %convert_element_type.37, () %tuple.29, (pred[64,8192]{1,0:T(8,128)(4,1)}, bf16[2,16,64,576]{3,1,2,0:T(8,128)(2,1)}, bf16[8192,576]{1,0:T(8,128)(2,1)}) %tuple.56), branch_computations={%region_1.2_spmd, %region_2.5_spmd} | conditional | flops 18320719872 | bytes 129912848 | solution.py:142
  146.9 2.3 copy.8
  149.3 22.3 %fusion = (f32[1024]{0:T(1024)S(1)}, f32[1024,8192]{1,0:T(8,128)}) fusion(pred[64,8192]{1,0:T(8,128)(4,1)} %get-tuple-element.25, bf16[1024,576]{1,0:T(8,128)(2,1)S(1)} %bitcast.59, bf16[8192,576]{1,0:T(8,128)(2,1)} %get-tuple-element.27), kind=kOutput, calls=%fused_computation.2 | convolution fusion | flops 9688841216 | bytes 44699648 | tf_op jit(solution)/shard_map/cond/branch_1_fun/dot_general | solution.py:120
  171.6 16.7 %fusion.1 = (bf16[1024,8192]{1,0:T(8,128)(2,1)S(1)}, f32[1024]{0:T(1024)S(1)}) fusion(f32[1024,8192]{1,0:T(8,128)} %get-tuple-element.52, f32[1024]{0:T(1024)S(1)} %broadcast_maximum_fusion, pred[64,8192]{1,0:T(8,128)(4,1)} %get-tuple-element.25), kind=kLoop, calls=%fused_computation.3 | loop fusion | flops 41942016 | bytes 50864128 | tf_op jit(solution)/shard_map/cond/branch_1_fun/convert_element_type | solution.py:135
  188.4 12.3 %fusion.3 = f32[1024,512]{1,0:T(8,128)} fusion(bf16[1024,8192]{1,0:T(8,128)(2,1)S(1)} %get-tuple-element.49, bf16[8192,576]{1,0:T(8,128)(2,1)} %get-tuple-element.27), kind=kOutput, calls=%fused_computation.5 | convolution fusion | flops 8589934592 | bytes 27262976 | tf_op jit(solution)/shard_map/cond/branch_1_fun/dot_general | solution.py:134
  200.7 53.9 %conditional.3 = (f32[1,1024]{1,0:T(1,128)S(1)}, f32[1,16,64,512]{3,2,1,0:T(8,128)}) conditional(s32[]{:T(128)} %convert_element_type.42, () %tuple.31, (pred[64,8192]{1,0:T(8,128)(4,1)}, bf16[2,16,64,576]{3,1,2,0:T(8,128)(2,1)}, bf16[8192,576]{1,0:T(8,128)(2,1)}) %tuple.57), branch_computations={%region_6.7_spmd, %region_7.10_spmd} | conditional | flops 18320719872 | bytes 129912848 | solution.py:142
  200.7 2.3 copy.9
  203.2 22.3 %fusion.5 = (f32[1024]{0:T(1024)S(1)}, f32[1024,8192]{1,0:T(8,128)}) fusion(pred[64,8192]{1,0:T(8,128)(4,1)} %get-tuple-element.28, bf16[1024,576]{1,0:T(8,128)(2,1)S(1)} %bitcast.60, bf16[8192,576]{1,0:T(8,128)(2,1)} %get-tuple-element.30), kind=kOutput, calls=%fused_computation.10 | convolution fusion | flops 9688841216 | bytes 44699648 | tf_op jit(solution)/shard_map/cond/branch_1_fun/dot_general | solution.py:120
  225.5 16.7 %fusion.6 = (bf16[1024,8192]{1,0:T(8,128)(2,1)S(1)}, f32[1024]{0:T(1024)S(1)}) fusion(f32[1024,8192]{1,0:T(8,128)} %get-tuple-element.56, f32[1024]{0:T(1024)S(1)} %broadcast_maximum_fusion.1, pred[64,8192]{1,0:T(8,128)(4,1)} %get-tuple-element.28), kind=kLoop, calls=%fused_computation.11 | loop fusion | flops 41942016 | bytes 50864128 | tf_op jit(solution)/shard_map/cond/branch_1_fun/convert_element_type | solution.py:135
  242.2 12.3 %fusion.8 = f32[1024,512]{1,0:T(8,128)} fusion(bf16[1024,8192]{1,0:T(8,128)(2,1)S(1)} %get-tuple-element.53, bf16[8192,576]{1,0:T(8,128)(2,1)} %get-tuple-element.30), kind=kOutput, calls=%fused_computation.13 | convolution fusion | flops 8589934592 | bytes 27262976 | tf_op jit(solution)/shard_map/cond/branch_1_fun/dot_general | solution.py:134
  254.7 3.0 %fusion.19 = bf16[2,64,16,128]{3,1,0,2:T(8,128)(2,1)S(1)} fusion(bf16[16,512,128]{2,1,0:T(8,128)(2,1)S(1)} %copy-done, f32[1,16,64,512]{3,2,1,0:T(8,128)} %get-tuple-element.36, f32[1,16,64,512]{3,2,1,0:T(8,128)} %get-tuple-element.35, f32[2,16,64]{2,1,0:T(8,128)S(1)} %div.37), kind=kOutput, calls=%fused_computation.25 | convolution fusion | flops 271843328 | bytes 6823936 | tf_op jit(solution)/shard_map/shcr,hrv->shcv/dot_general | solution.py:150
  258.0 0.9 copy.21
  (26 shorter events, 2.3 us)
Async XLA Ops:
  6.5 248.1 %copy-start = (bf16[16,512,128]{2,1,0:T(8,128)(2,1)S(1)}, bf16[16,512,128]{2,1,0:T(8,128)(2,1)}, u32[]{:S(2)}) copy-start(bf16[16,512,128]{2,1,0:T(8,128)(2,1)} %param.11) | copy-start | bytes 6291460
  6.5 140.3 %all-gather.2.cloned.1.call-start = ((), (), s32[]{:S(2)}) async-start(), calls=%async_computation.1 | async-start | bytes 10649600 | tf_op jit(solution)/shard_map/all_gather | solution.py:103
Sparse Core Ops, SparseCore 0:
  21.5 125.3 all-gather.1
where the time goes:
time: 266 us
  waiting for transfers between devices  106 us (40%)
  matrix products  72.3 us (27%)
  other arithmetic  42.1 us (16%)
  local copies, waits for them, and re-layouts  18.8 us (7%)
  between operations  14.7 us (6%)
  blocking collectives  12 us (5%)
    all_gather x1, waiting for transfers between devices, per_device(): shard_rows = lax.all_gather(group_rows, 'seq', axis=0, tiled=True)  106 us
    dot_general x2, matrix products, update(): lax.dot_general(block_rows, shard_rows, (((1,), (1,)), ((), ())), preferr...  44.6 us
    convert_element_type x2, other arithmetic, update(): expo.astype(jnp.bfloat16)  33.5 us
    dot_general x2, matrix products, update(): jnp.dot(expo.astype(jnp.bfloat16), shard_rows[:, :latent_rank], preferred...  24.7 us
    all_to_all x1, blocking collectives, copy_for_each(): return lax.all_to_all(copies, axis, split_axis=0, concat_axis=0, tiled=True)  12 us
  transfers between devices with their start and end apart: 1, of which 1 were waited for; matrix products, arithmetic and copies ran while one was open for 7% of the time, Pallas kernels for 0%

commit v1 on v0

--- a/solution.py
+++ b/solution.py
@@ -100,7 +100,9 @@
     span_seq = query_seq.reshape(2, span_len)[:, 0]
     logit_scale_factor = (NOPE_DIM + ROPE_DIM) ** (-0.5)
     group_rows = collect(key_rows, "head", 0)
-    shard_rows = lax.all_gather(group_rows, "seq", axis=0, tiled=True)
+    shard_rows = jnp.concatenate(
+        lax.all_to_all(jnp.stack([group_rows] * lax.axis_size("seq")), "seq", 0, 0), axis=0
+    )
     row_count = shard_rows.shape[0]
     maxima = jnp.full((2, head_count * span_len), floor_score, jnp.float32)
     totals = jnp.zeros((2, head_count * span_len), jnp.float32)

time: 266 us -> 414 us (1.56)
  waiting for transfers between devices: 106 us -> 191 us
  local copies, waits for them, and re-layouts: 18.8 us -> 61.7 us
  starting transfers between devices: 0.01 us -> 13.8 us
  between operations: 14.7 us -> 1.38 us
  other arithmetic: 42.1 us -> 52.5 us
  matrix products: 72.3 us -> 79.6 us
    all_to_all x0 -> x1, waiting for transfers between devices: none -> 191 us  [per_device(): lax.all_to_all(jnp.stack([group_rows] * lax.axis_size('seq')), 'seq', 0, 0)]
    all_gather x1 -> x0, waiting for transfers between devices: 106 us -> none  [per_device(): shard_rows = lax.all_gather(group_rows, 'seq', axis=0, tiled=True)]
    another operation x2 -> x6, local copies, waits for them, and re-layouts: 4.69 us -> 38.9 us
    all_to_all x0 -> x1, starting transfers between devices: none -> 13.8 us  [per_device(): lax.all_to_all(jnp.stack([group_rows] * lax.axis_size('seq')), 'seq', 0, 0)]
    convert_element_type x2, other arithmetic: 33.5 us -> 44.4 us  [update(): expo.astype(jnp.bfloat16)]
    reshape x0 -> x1, local copies, waits for them, and re-layouts: none -> 8.63 us  [per_device(): jnp.concatenate(lax.all_to_all(jnp.stack([group_rows] * lax.axis_size('se...]
    dot_general x2, matrix products: 24.7 us -> 31.5 us  [update(): jnp.dot(expo.astype(jnp.bfloat16), shard_rows[:, :latent_rank], preferred...]
  transfers between devices with their start and end apart: 1 -> 1, of which waited for: 1 -> 1; matrix products, arithmetic and copies ran while one was open for 7% -> 4% of each run, Pallas kernels for 0% -> 0%
where the time goes in v1:
time: 414 us; the launch traced here: 412 us
  waiting for transfers between devices  191 us (46%)
  matrix products  79.6 us (19%)
  local copies, waits for them, and re-layouts  61.7 us (15%)
  other arithmetic  52.5 us (13%)
  starting transfers between devices  13.8 us (3%)
  blocking collectives  11.9 us (3%)
    all_to_all x1, waiting for transfers between devices, per_device(): lax.all_to_all(jnp.stack([group_rows] * lax.axis_size('seq')), 'seq', 0, 0)  191 us
    dot_general x2, matrix products, update(): lax.dot_general(block_rows, shard_rows, (((1,), (1,)), ((), ())), preferr...  45.2 us
    convert_element_type x2, other arithmetic, update(): expo.astype(jnp.bfloat16)  44.4 us
    another operation x4, local copies, waits for them, and re-layouts  32.8 us
    dot_general x2, matrix products, update(): jnp.dot(expo.astype(jnp.bfloat16), shard_rows[:, :latent_rank], preferred...  31.5 us
    all_to_all x1, starting transfers between devices, per_device(): lax.all_to_all(jnp.stack([group_rows] * lax.axis_size('seq')), 'seq', 0, 0)  13.8 us
    all_to_all x1, blocking collectives, copy_for_each(): return lax.all_to_all(copies, axis, split_axis=0, concat_axis=0, tiled=True)  11.9 us
    reshape x1, local copies, waits for them, and re-layouts, per_device(): jnp.concatenate(lax.all_to_all(jnp.stack([group_rows] * lax.axis_size('se...  8.63 us
  transfers between devices with their start and end apart: 1, of which 1 were waited for; matrix products, arithmetic and copies ran while one was open for 4% of the time, Pallas kernels for 0%

profile of v1, /device:TPU:1, one launch (start us, length us, event | category | flops | bytes accessed | tf_op | source)
XLA Modules:
  0.0 412.0 jit_solution(5340027363032271295)
XLA Ops:
  2.8 11.9 %all_to_all.10 = bf16[4,32,576]{2,1,0:T(8,128)(2,1)S(1)} all-to-all(bf16[4,32,576]{2,1,0:T(8,128)(2,1)S(1)} %broadcast_in_dim.44), channel_id=1, replica_groups=mesh['seq'=64,'head'=4] {'head'}, dimensions={0} | all-to-all | bytes 294912 | tf_op jit(solution)/shard_map/all_to_all | solution.py:16
  14.9 5.9 %stack.33 = bf16[64,128,576]{1,2,0:T(8,128)(2,1)} broadcast(bf16[128,576]{0,1:T(8,128)(2,1)S(1)} %copy.21), dimensions={1,2} | broadcast | bytes 9584640 | tf_op jit(solution)/shard_map/stack | solution.py:104
  20.8 13.8 %all-to-all-start.1 = ((bf16[64,128,576]{1,2,0:T(8,128)(2,1)}), bf16[64,128,576]{1,2,0:T(8,128)(2,1)}, u32[]{:S(2)}, u32[]{:S(2)}) async-start(bf16[64,128,576]{1,2,0:T(8,128)(2,1)} %stack.33), calls=%async_computation.1 | async-start | bytes 18874368 | tf_op jit(solution)/shard_map/all_to_all | solution.py:104
  34.8 4.3 %copy.19 = bf16[128,9216]{0,1:T(8,128)(2,1)} copy(bf16[128,9216]{1,0:T(8,128)(2,1)} %param.9) | data formatting | bytes 4718592 | tf_op args[1]
  39.1 1.7 slice.75
  42.1 1.6 pad_maximum_fusion
  43.7 4.9 %copy.20 = bf16[128,16,576]{2,1,0:T(8,128)(2,1)} copy(bf16[128,16,576]{0,2,1:T(8,128)(2,1)} %pad_maximum_fusion) | data formatting | bytes 4718592 | tf_op jit(solution)/shard_map/concatenate | solution.py:93
  49.2 1.3 broadcast_compare_fusion
  50.5 2.0 fusion.34
  53.8 191.1 %all-to-all-done.1 = bf16[64,128,576]{1,2,0:T(8,128)(2,1)} async-done(((bf16[64,128,576]{1,2,0:T(8,128)(2,1)}), bf16[64,128,576]{1,2,0:T(8,128)(2,1)}, u32[]{:S(2)}, u32[]{:S(2)}) %all-to-all-start.1) | async-done | bytes 9437216 | tf_op jit(solution)/shard_map/all_to_all | solution.py:104
  244.8 8.6 %copy_bitcast_fusion = bf16[8192,576]{0,1:T(8,128)(2,1)} fusion(bf16[64,128,576]{1,2,0:T(8,128)(2,1)} %all-to-all-done.1), kind=kLoop, calls=%fused_computation.16 | loop fusion | bytes 18874368 | tf_op jit(solution)/shard_map/reshape | solution.py:103
  253.4 77.1 %conditional.2 = (f32[1,1024]{1,0:T(1,128)S(1)}, f32[1,16,64,512]{3,2,1,0:T(8,128)}) conditional(s32[]{:T(128)} %convert_element_type.37, () %tuple.29, (pred[64,8192]{1,0:T(8,128)(4,1)S(1)}, bf16[2,16,64,576]{3,1,2,0:T(8,128)(2,1)}, bf16[8192,576]{0,1:T(8,128)(2,1)}) %tuple.58), branch_computations={%region_1.2_spmd, %region_2.5_spmd} | conditional | flops 18320719872 | bytes 148787216 | solution.py:144
  253.4 2.3 copy.23
  255.9 22.6 %fusion = (f32[1024]{0:T(1024)S(1)}, f32[1024,8192]{1,0:T(8,128)}) fusion(pred[64,8192]{1,0:T(8,128)(4,1)S(1)} %get-tuple-element.25, bf16[1024,576]{1,0:T(8,128)(2,1)S(1)} %bitcast.64, bf16[8192,576]{0,1:T(8,128)(2,1)} %get-tuple-element.53), kind=kOutput, calls=%fused_computation.2 | convolution fusion | flops 9688841216 | bytes 44699648 | tf_op jit(solution)/shard_map/cond/branch_1_fun/dot_general | solution.py:122
  278.5 22.2 %fusion.1 = (bf16[1024,8192]{1,0:T(8,128)(2,1)}, f32[1024]{0:T(1024)S(1)}) fusion(f32[1024,8192]{1,0:T(8,128)} %get-tuple-element.64, f32[1024]{0:T(1024)S(1)} %broadcast_maximum_fusion, pred[64,8192]{1,0:T(8,128)(4,1)S(1)} %get-tuple-element.25), kind=kLoop, calls=%fused_computation.3 | loop fusion | flops 41942016 | bytes 50864128 | tf_op jit(solution)/shard_map/cond/branch_1_fun/convert_element_type | solution.py:137
  300.7 14.1 %copy.24 = bf16[8192,576]{1,0:T(8,128)(2,1)} copy(bf16[8192,576]{0,1:T(8,128)(2,1)} %get-tuple-element.53) | data formatting | bytes 18874368 | tf_op jit(solution)/shard_map
  314.8 15.7 %fusion.3 = f32[1024,512]{1,0:T(8,128)} fusion(bf16[1024,8192]{1,0:T(8,128)(2,1)} %get-tuple-element.61, bf16[8192,576]{1,0:T(8,128)(2,1)} %copy.24), kind=kOutput, calls=%fused_computation.5 | convolution fusion | flops 8589934592 | bytes 27262976 | tf_op jit(solution)/shard_map/cond/branch_1_fun/dot_general | solution.py:136
  330.5 77.1 %conditional.3 = (f32[1,1024]{1,0:T(1,128)S(1)}, f32[1,16,64,512]{3,2,1,0:T(8,128)}) conditional(s32[]{:T(128)} %convert_element_type.42, () %tuple.31, (pred[64,8192]{1,0:T(8,128)(4,1)S(1)}, bf16[2,16,64,576]{3,1,2,0:T(8,128)(2,1)}, bf16[8192,576]{0,1:T(8,128)(2,1)}) %tuple.59), branch_computations={%region_6.7_spmd, %region_7.10_spmd} | conditional | flops 18320719872 | bytes 148787216 | solution.py:144
  330.5 2.3 copy.25
  333.0 22.6 %fusion.5 = (f32[1024]{0:T(1024)S(1)}, f32[1024,8192]{1,0:T(8,128)}) fusion(pred[64,8192]{1,0:T(8,128)(4,1)S(1)} %get-tuple-element.28, bf16[1024,576]{1,0:T(8,128)(2,1)S(1)} %bitcast.65, bf16[8192,576]{0,1:T(8,128)(2,1)} %get-tuple-element.56), kind=kOutput, calls=%fused_computation.10 | convolution fusion | flops 9688841216 | bytes 44699648 | tf_op jit(solution)/shard_map/cond/branch_1_fun/dot_general | solution.py:122
  355.6 22.2 %fusion.6 = (bf16[1024,8192]{1,0:T(8,128)(2,1)}, f32[1024]{0:T(1024)S(1)}) fusion(f32[1024,8192]{1,0:T(8,128)} %get-tuple-element.68, f32[1024]{0:T(1024)S(1)} %broadcast_maximum_fusion.1, pred[64,8192]{1,0:T(8,128)(4,1)S(1)} %get-tuple-element.28), kind=kLoop, calls=%fused_computation.11 | loop fusion | flops 41942016 | bytes 50864128 | tf_op jit(solution)/shard_map/cond/branch_1_fun/convert_element_type | solution.py:137
  377.8 14.1 %copy.26 = bf16[8192,576]{1,0:T(8,128)(2,1)} copy(bf16[8192,576]{0,1:T(8,128)(2,1)} %get-tuple-element.56) | data formatting | bytes 18874368 | tf_op jit(solution)/shard_map
  391.9 15.7 %fusion.8 = f32[1024,512]{1,0:T(8,128)} fusion(bf16[1024,8192]{1,0:T(8,128)(2,1)} %get-tuple-element.65, bf16[8192,576]{1,0:T(8,128)(2,1)} %copy.26), kind=kOutput, calls=%fused_computation.13 | convolution fusion | flops 8589934592 | bytes 27262976 | tf_op jit(solution)/shard_map/cond/branch_1_fun/dot_general | solution.py:136
  407.7 3.0 fusion.19
  (30 shorter events, 6.6 us)
Async XLA Ops:
  0.0 407.7 %copy-start = (bf16[16,512,128]{2,1,0:T(8,128)(2,1)S(1)}, bf16[16,512,128]{2,1,0:T(8,128)(2,1)}, u32[]{:S(2)}) copy-start(bf16[16,512,128]{2,1,0:T(8,128)(2,1)} %param.11) | copy-start | bytes 6291460
  20.8 224.0 %all-to-all-start.1 = ((bf16[64,128,576]{1,2,0:T(8,128)(2,1)}), bf16[64,128,576]{1,2,0:T(8,128)(2,1)}, u32[]{:S(2)}, u32[]{:S(2)}) async-start(bf16[64,128,576]{1,2,0:T(8,128)(2,1)} %stack.33), calls=%async_computation.1 | async-start | bytes 18874368 | tf_op jit(solution)/shard_map/all_to_all | solution.py:104
